TPU v7x, 32 devices: a whole 2x2x4 slice. The times are simulated.
32 devices in a mesh: dp: 8 (over z, x), mp: 4 (over y, core).
Axes of the slice: x: 2, y: 2, z: 4, core: 2. Of those that a mesh axis runs over, the one named last changes fastest.
Arguments:
- tokens: bfloat16 [8192, 2048], P('dp', 'mp'), may hold values from -6 to 6
- norm_gain: bfloat16 [2048], replicated, may hold values from 0.099609375 to 1.8984375
- wi_gate: bfloat16 [2048, 5120], P(None, 'mp'), may hold values from -0.125 to 0.125
- wi_linear: bfloat16 [2048, 5120], P(None, 'mp'), may hold values from -0.125 to 0.125
- wo_out: bfloat16 [5120, 2048], P('mp'), may hold values from -0.078125 to 0.078125
- task_table: float32 [8, 64], replicated, may hold values from -5 to 5
- layer_table: float32 [24, 64], replicated, may hold values from -5 to 5
- task_ids: int32 [64], P('dp'), may hold values from 0 to 7
- layer_index: int32 [1], replicated, may hold values from 0 to 23
- hyper_in: bfloat16 [128, 1024], P(None, 'mp'), may hold values from -0.5 to 0.5
- gen_down: bfloat16 [1024, 131072], P(None, ('mp', 'dp')), may hold values from -0.0078125 to 0.0078125
- gen_up: bfloat16 [1024, 131072], P(None, ('mp', 'dp')), may hold values from -0.046875 to 0.046875
Outputs:
- mixed: bfloat16 [8192, 2048], P('dp', 'mp')
All inputs are finite; a program needn't handle non-finite values.
Results may differ from a plain program's by a relative error of at most 0.019.
Values may be sent and summed in bfloat16 or wider, within the bound.
A program may use at most 128 MiB of HBM per device.

v0:
```python
import jax
import jax.numpy as jnp
from jax import lax
from jax.sharding import PartitionSpec as P

R = 64


def matmul(left, right):
    return jnp.dot(left, right, preferred_element_type=jnp.float32)


def per_device(
    tokens,
    norm_gain,
    wi_gate,
    wi_linear,
    wo_out,
    task_table,
    layer_table,
    task_ids,
    layer_index,
    hyper_in,
    gen_down,
    gen_up,
):
    task_count = task_table.shape[0]
    layer_row = jnp.take(layer_table, layer_index, axis=0)
    embed = jnp.concatenate(
        [task_table, jnp.broadcast_to(layer_row, (task_count, layer_row.shape[1]))], axis=1
    ).astype(jnp.bfloat16)
    hidden_part = jnp.maximum(matmul(embed, hyper_in), 0.0).astype(jnp.bfloat16)
    hidden = lax.all_gather(hidden_part, "mp", axis=1, tiled=True)
    every_id = lax.all_gather(task_ids, "dp", axis=0, tiled=True)
    wanted = jnp.take(hidden, every_id, axis=0)
    made = (
        matmul(wanted, gen_down).astype(jnp.bfloat16),
        matmul(wanted, gen_up).astype(jnp.bfloat16),
    )
    local_down, local_up = (
        lax.all_to_all(made[0], "dp", split_axis=0, concat_axis=1, tiled=True),
        lax.all_to_all(made[1], "dp", split_axis=0, concat_axis=1, tiled=True),
    )
    full_rows = lax.all_gather(tokens, "mp", axis=1, tiled=True)
    wide = full_rows.astype(jnp.float32)
    scale = lax.rsqrt(jnp.mean(wide * wide, axis=-1, keepdims=True) + 1e-06)
    normed = (wide * scale * norm_gain.astype(jnp.float32)).astype(jnp.bfloat16)
    gate = matmul(normed, wi_gate)
    linear = matmul(normed, wi_linear)
    act = (jax.nn.gelu(gate, approximate=True) * linear).astype(jnp.bfloat16)
    seqs_dev = task_ids.shape[0]
    tok_dev = tokens.shape[0]
    seq_len = tok_dev // seqs_dev
    partial_sums = matmul(act, wo_out)
    ffout = lax.psum_scatter(
        partial_sums.astype(jnp.bfloat16), "mp", scatter_dimension=1, tiled=True
    )
    down_block = local_down.reshape(seqs_dev, -1, R)
    up_block = local_up.reshape(seqs_dev, -1, R)
    blocks = ffout.reshape(seqs_dev, seq_len, -1)
    squeeze_part = jnp.einsum(
        "std,sdr->str", blocks, down_block, preferred_element_type=jnp.float32
    )
    squeeze_full = lax.psum(squeeze_part.astype(jnp.bfloat16), "mp").astype(jnp.float32)
    squeezed = jnp.maximum(squeeze_full, 0.0).astype(jnp.bfloat16)
    expand = jnp.einsum("str,sdr->std", squeezed, up_block, preferred_element_type=jnp.float32)
    total = tokens.astype(jnp.float32) + ffout.astype(jnp.float32) + expand.reshape(tok_dev, -1)
    return total.astype(jnp.bfloat16)


def solution(mesh):
    return jax.shard_map(
        per_device,
        mesh=mesh,
        in_specs=(
            P("dp", "mp"),
            P(),
            P(None, "mp"),
            P(None, "mp"),
            P("mp", None),
            P(),
            P(),
            P("dp"),
            P(),
            P(None, "mp"),
            P(None, ("mp", "dp")),
            P(None, ("mp", "dp")),
        ),
        out_specs=P("dp", "mp"),
        check_vma=False,
    )
```

profile of v0, /device:TPU:0, one launch (start us, length us, event | category | flops | bytes accessed | tf_op | source)
XLA Modules:
  0.0 174.6 jit_solution(7065484068272233757)
XLA Ops:
  6.5 0.7 all-gather.2.cloned.1.call-update
  7.3 0.0 reduce-scatter.2.cloned.1.call-start
  7.3 0.7 convert_element_type.45
  8.0 38.1 %all-gather.2.cloned.1.call-done = bf16[1024,2048]{1,0:T(8,128)(2,1)} async-done(((bf16[1024,512]{1,0:T(8,128)(2,1)}), bf16[1024,2048]{1,0:T(8,128)(2,1)}) %all-gather.2.cloned.1.call-update) | async-done | bytes 4194320 | tf_op jit(solution)/shard_map/all_gather | solution.py:44
  46.1 3.1 %fusion = f32[1024]{0:T(1024)S(1)} fusion(bf16[1024,2048]{1,0:T(8,128)(2,1)} %all-gather.2.cloned.1.call-done), kind=kLoop, calls=%fused_computation.3 | loop fusion | flops 6290432 | bytes 4198400 | tf_op jit(solution)/shard_map/reduce_sum | solution.py:46
  49.2 10.7 %fusion.16 = f32[1024,1280]{1,0:T(8,128)} fusion(bf16[2048,1280]{1,0:T(8,128)(2,1)} %param.14, bf16[1024,2048]{1,0:T(8,128)(2,1)} %all-gather.2.cloned.1.call-done, f32[2048]{0:T(1024)S(1)} %convert_element_type.45, f32[1024]{0:T(1024)S(1)} %add_rsqrt_fusion), kind=kOutput, calls=%fused_computation.23 | convolution fusion | flops 5377097728 | bytes 14692352 | tf_op jit(solution)/shard_map/dot_general | solution.py:10
  59.9 19.9 %convolution_convert_fusion.2 = bf16[1024,2048]{1,0:T(8,128)(2,1)} fusion(bf16[1280,2048]{1,0:T(8,128)(2,1)} %param.16, f32[1024,1280]{1,0:T(8,128)} %fusion.16, bf16[2048,1280]{1,0:T(8,128)(2,1)} %param.15, bf16[1024,2048]{1,0:T(8,128)(2,1)} %all-gather.2.cloned.1.call-done, f32[2048]{0:T(1024)S(1)} %convert_element_type.45, f32[1024]{0:T(1024)S(1)} %add_rsqrt_fusion), kind=kOutput, calls=%fused_computation.20 | convolution fusion | flops 10761011200 | bytes 24129536 | tf_op jit(solution)/shard_map/dot_general | solution.py:10
  79.8 0.0 reduce-scatter.2.cloned.1.call-update
  80.5 0.7 fusion.27
  81.2 0.1 pad.3.clone
  81.3 0.6 dynamic-slice.4
  82.6 0.2 dynamic-update-slice.1
  82.8 11.4 %all-reduce = s32[64]{0:T(128)S(1)} all-reduce(s32[64]{0:T(128)S(1)} %dynamic-update-slice.1), channel_id=1, replica_groups=mesh['dp'=8,'mp'=4] {'dp'}, use_global_device_ids=true, to_apply=%add | all-reduce | flops 64 | bytes 512
  94.2 0.1 fusion.18
  94.3 5.2 %all_gather.11 = bf16[8,1024]{1,0:T(8,128)(2,1)S(1)} all-gather(bf16[8,256]{1,0:T(8,128)(2,1)S(1)} %fusion.18), channel_id=1, replica_groups=mesh['dp'=8,'mp'=4] {'mp'}, dimensions={1}, use_global_device_ids=true | all-gather | bytes 20480 | tf_op jit(solution)/shard_map/all_gather | solution.py:33
  99.5 0.7 gather_fusion
  100.2 5.8 %fusion.12 = bf16[8,8,4096]{2,1,0:T(8,128)(2,1)} fusion(bf16[1024,4096]{1,0:T(8,128)(2,1)} %param.22, bf16[64,1024]{1,0:T(8,128)(2,1)S(1)} %gather_fusion, pred[64]{0:T(512)(128)(4,1)S(1)} %compare_and_fusion), kind=kOutput, calls=%fused_computation.18 | convolution fusion | flops 537198592 | bytes 9044032 | tf_op jit(solution)/shard_map/dot_general | solution.py:10
  106.1 3.5 %all-to-all-start = ((bf16[8,8,4096]{2,1,0:T(8,128)(2,1)}), bf16[8,8,4096]{2,1,0:T(8,128)(2,1)S(1)}, u32[]{:S(2)}, u32[]{:S(2)}) async-start(bf16[8,8,4096]{2,1,0:T(8,128)(2,1)} %fusion.12), calls=%async_computation.1 | async-start | bytes 1048576 | tf_op jit(solution)/shard_map/all_to_all | solution.py:41
  109.6 5.8 %fusion.13 = bf16[8,8,4096]{2,1,0:T(8,128)(2,1)} fusion(bf16[1024,4096]{1,0:T(8,128)(2,1)} %param.23, bf16[64,1024]{1,0:T(8,128)(2,1)S(1)} %gather_fusion, pred[64]{0:T(512)(128)(4,1)S(1)} %compare_and_fusion), kind=kOutput, calls=%fused_computation.19 | convolution fusion | flops 537198592 | bytes 9044032 | tf_op jit(solution)/shard_map/dot_general | solution.py:10
  115.4 9.4 %all-to-all-done = bf16[8,8,4096]{2,1,0:T(8,128)(2,1)S(1)} async-done(((bf16[8,8,4096]{2,1,0:T(8,128)(2,1)}), bf16[8,8,4096]{2,1,0:T(8,128)(2,1)S(1)}, u32[]{:S(2)}, u32[]{:S(2)}) %all-to-all-start) | async-done | bytes 524320 | tf_op jit(solution)/shard_map/all_to_all | solution.py:41
  124.8 4.3 %all-to-all-start.1 = ((bf16[8,8,4096]{2,1,0:T(8,128)(2,1)}), bf16[8,8,4096]{2,1,0:T(8,128)(2,1)}, u32[]{:S(2)}, u32[]{:S(2)}) async-start(bf16[8,8,4096]{2,1,0:T(8,128)(2,1)} %fusion.13), calls=%async_computation.2 | async-start | bytes 1048576 | tf_op jit(solution)/shard_map/all_to_all | solution.py:42
  129.1 0.0 all-reduce.3.cloned.1.call-start
  129.1 0.3 copy.16
  129.4 1.1 reshape.46
  130.6 0.0 reduce-scatter.2.cloned.1.call-done
  130.6 2.5 %convolution_convert_fusion.3 = bf16[8,128,64]{1,2,0:T(8,128)(2,1)} fusion(bf16[8,128,512]{2,1,0:T(8,128)(2,1)} %bitcast.25, bf16[8,512,64]{2,1,0:T(8,128)(2,1)S(1)} %reshape.46), kind=kOutput, calls=%fused_computation.24 | convolution fusion | flops 67174400 | bytes 1703936 | tf_op jit(solution)/shard_map/std,sdr->str/dot_general | solution.py:61
  133.1 10.2 %all-to-all-done.1 = bf16[8,8,4096]{2,1,0:T(8,128)(2,1)} async-done(((bf16[8,8,4096]{2,1,0:T(8,128)(2,1)}), bf16[8,8,4096]{2,1,0:T(8,128)(2,1)}, u32[]{:S(2)}, u32[]{:S(2)}) %all-to-all-start.1) | async-done | bytes 524320 | tf_op jit(solution)/shard_map/all_to_all | solution.py:42
  143.3 2.1 %copy.18 = bf16[8,8,4096]{2,1,0:T(8,128)(2,1)} copy(bf16[8,8,4096]{2,0,1:T(8,128)(2,1)} %bitcast.8) | data formatting | bytes 1048576 | tf_op jit(solution)/shard_map/all_to_all | solution.py:42
  145.4 2.1 %reshape.47 = bf16[8,512,64]{2,1,0:T(8,128)(2,1)S(1)} reshape(bf16[8,8,4096]{2,1,0:T(8,128)(2,1)} %copy.18) | data formatting | bytes 1048576 | tf_op jit(solution)/shard_map/reshape | solution.py:59
  147.5 17.7 %all-reduce.3.cloned.1.call-done = bf16[8,128,64]{1,2,0:T(8,128)(2,1)} async-done(((bf16[8,128,64]{1,2,0:T(8,128)(2,1)}), bf16[8,128,64]{1,2,0:T(8,128)(2,1)}) %all-reduce.3.cloned.1.call-update) | async-done | bytes 131088 | tf_op jit(solution)/shard_map/psum | solution.py:64
  165.2 1.4 fusion.21
  166.6 1.4 fusion.14
  (20 shorter events, 0.1 us)
Async XLA Ops:
  6.5 87.6 %copy-start = (bf16[128,256]{1,0:T(8,128)(2,1)S(1)}, bf16[128,256]{1,0:T(8,128)(2,1)}, u32[]{:S(2)}) copy-start(bf16[128,256]{1,0:T(8,128)(2,1)} %param.21) | copy-start | bytes 196612
  6.5 39.6 %all-gather.2.cloned.1.call-start = ((), (), s32[]{:S(2)}) async-start(), calls=%async_computation.3 | async-start | bytes 5242880 | tf_op jit(solution)/shard_map/all_gather | solution.py:44
  7.3 123.3 %reduce-scatter.2.cloned.1.call-start = ((), (), s32[]{:S(2)}) async-start(), calls=%async_computation.4 | async-start | bytes 5242880 | tf_op jit(solution)/shard_map/reduce_scatter | solution.py:55
  59.9 20.6 %copy-start.3 = (f32[8,64]{1,0:T(8,128)S(1)}, f32[8,64]{1,0:T(8,128)}, u32[]{:S(2)}) copy-start(f32[8,64]{1,0:T(8,128)} %param.17) | copy-start | bytes 6148
  59.9 21.4 %copy-start.5 = (u32[32]{0:T(128)S(1)}, u32[32]{0:T(128)}, u32[]{:S(2)}) copy-start(u32[32]{0:T(128)} %constant.73) | copy-start | bytes 388
  59.9 22.7 %copy-start.4 = (s32[8]{0:T(128)S(1)}, s32[8]{0:T(128)}, u32[]{:S(2)}) copy-start(s32[8]{0:T(128)} %param.19) | copy-start | bytes 100
  106.1 18.7 %all-to-all-start = ((bf16[8,8,4096]{2,1,0:T(8,128)(2,1)}), bf16[8,8,4096]{2,1,0:T(8,128)(2,1)S(1)}, u32[]{:S(2)}, u32[]{:S(2)}) async-start(bf16[8,8,4096]{2,1,0:T(8,128)(2,1)} %fusion.12), calls=%async_computation.1 | async-start | bytes 1048576 | tf_op jit(solution)/shard_map/all_to_all | solution.py:41
  124.8 18.6 %all-to-all-start.1 = ((bf16[8,8,4096]{2,1,0:T(8,128)(2,1)}), bf16[8,8,4096]{2,1,0:T(8,128)(2,1)}, u32[]{:S(2)}, u32[]{:S(2)}) async-start(bf16[8,8,4096]{2,1,0:T(8,128)(2,1)} %fusion.13), calls=%async_computation.2 | async-start | bytes 1048576 | tf_op jit(solution)/shard_map/all_to_all | solution.py:42
  129.1 36.1 %all-reduce.3.cloned.1.call-start = ((), (), s32[]{:S(2)}) async-start(), calls=%async_computation.5 | async-start | bytes 262144 | tf_op jit(solution)/shard_map/psum | solution.py:64
  129.1 37.5 %copy-start.1 = (bf16[1024,512]{1,0:T(8,128)(2,1)S(1)}, bf16[1024,512]{1,0:T(8,128)(2,1)}, u32[]{:S(2)}) copy-start(bf16[1024,512]{1,0:T(8,128)(2,1)} %param.12) | copy-start | bytes 3145732
  130.6 36.0 %copy-start.2 = (bf16[1024,512]{1,0:T(8,128)(2,1)S(1)}, bf16[1024,512]{1,0:T(8,128)(2,1)}, u32[]{:S(2)}) copy-start(bf16[1024,512]{1,0:T(8,128)(2,1)} %reduce-scatter.2.cloned.1.call-done) | copy-start | bytes 3145732
Sparse Core Ops, SparseCore 0:
  8.9 37.1 all-gather.1
  80.0 44.3 reduce-scatter.1
  133.2 31.9 all-reduce.2
where the time goes:
time: 175 us
  waiting for transfers between devices  76.2 us (44%)
  matrix products  46.2 us (26%)
  blocking collectives  16.6 us (9%)
  between operations  14.6 us (8%)
  starting transfers between devices  7.9 us (5%)
  local copies, waits for them, and re-layouts  7.23 us (4%)
  other arithmetic  5.92 us (3%)
    dot_general x5, matrix products, matmul(): return jnp.dot(left, right, preferred_element_type=jnp.float32)  42.4 us
    all_gather x1, waiting for transfers between devices, per_device(): full_rows = lax.all_gather(tokens, 'mp', axis=1, tiled=True)  38.1 us
    psum x1, waiting for transfers between devices, per_device(): lax.psum(squeeze_part.astype(jnp.bfloat16), 'mp').astype(jnp.float32)  17.7 us
    unnamed x1, blocking collectives  11.4 us
    all_to_all x1, waiting for transfers between devices, per_device(): lax.all_to_all(made[1], 'dp', split_axis=0, concat_axis=1, tiled=True)  10.2 us
    all_to_all x1, waiting for transfers between devices, per_device(): lax.all_to_all(made[0], 'dp', split_axis=0, concat_axis=1, tiled=True)  9.39 us
    all_gather x1, blocking collectives, per_device(): hidden = lax.all_gather(hidden_part, 'mp', axis=1, tiled=True)  5.2 us
    all_to_all x1, starting transfers between devices, per_device(): lax.all_to_all(made[1], 'dp', split_axis=0, concat_axis=1, tiled=True)  4.33 us
  transfers between devices with their start and end apart: 5, of which 4 were waited for; matrix products, arithmetic and copies ran while one was open for 13% of the time, Pallas kernels for 0%

commit v1 on v0

--- a/solution.py
+++ b/solution.py
@@ -4,6 +4,11 @@
 from jax.sharding import PartitionSpec as P
 
 R = 64
+
+
+def gather_and_add(x, axis):
+    shards = lax.all_gather(x, axis)
+    return jnp.sum(shards, axis=0)
 
 
 def matmul(left, right):
@@ -61,7 +66,7 @@
     squeeze_part = jnp.einsum(
         "std,sdr->str", blocks, down_block, preferred_element_type=jnp.float32
     )
-    squeeze_full = lax.psum(squeeze_part.astype(jnp.bfloat16), "mp").astype(jnp.float32)
+    squeeze_full = gather_and_add(squeeze_part.astype(jnp.bfloat16), "mp").astype(jnp.float32)
     squeezed = jnp.maximum(squeeze_full, 0.0).astype(jnp.bfloat16)
     expand = jnp.einsum("str,sdr->std", squeezed, up_block, preferred_element_type=jnp.float32)
     total = tokens.astype(jnp.float32) + ffout.astype(jnp.float32) + expand.reshape(tok_dev, -1)

time: 175 us -> 164 us (0.937)
  waiting for transfers between devices: 76.2 us -> 60.5 us
  blocking collectives: 16.6 us -> 23.5 us
  local copies, waits for them, and re-layouts: 7.23 us -> 5.43 us
    psum x1 -> x0, waiting for transfers between devices: 17.7 us -> none  [per_device(): lax.psum(squeeze_part.astype(jnp.bfloat16), 'mp').astype(jnp.float32)]
    all_gather x0 -> x1, blocking collectives: none -> 6.95 us  [gather_and_add(): shards = lax.all_gather(x, axis)]
    all_to_all x1, waiting for transfers between devices: 10.2 us -> 12.2 us  [per_device(): lax.all_to_all(made[1], 'dp', split_axis=0, concat_axis=1, tiled=True)]
    all_to_all x1, local copies, waits for them, and re-layouts: 2.13 us -> 0.29 us  [per_device(): lax.all_to_all(made[1], 'dp', split_axis=0, concat_axis=1, tiled=True)]
  transfers between devices with their start and end apart: 5 -> 4, of which waited for: 4 -> 3; matrix products, arithmetic and copies ran while one was open for 13% -> 11% of each run, Pallas kernels for 0% -> 0%
where the time goes in v1:
time: 164 us
  waiting for transfers between devices  60.5 us (37%)
  matrix products  45 us (27%)
  blocking collectives  23.5 us (14%)
  between operations  14.9 us (9%)
  starting transfers between devices  7.21 us (4%)
  other arithmetic  7.04 us (4%)
  local copies, waits for them, and re-layouts  5.43 us (3%)
    dot_general x5, matrix products, matmul(): return jnp.dot(left, right, preferred_element_type=jnp.float32)  42.4 us
    all_gather x1, waiting for transfers between devices, per_device(): full_rows = lax.all_gather(tokens, 'mp', axis=1, tiled=True)  38.1 us
    all_to_all x1, waiting for transfers between devices, per_device(): lax.all_to_all(made[1], 'dp', split_axis=0, concat_axis=1, tiled=True)  12.2 us
    unnamed x1, blocking collectives  11.3 us
    all_to_all x1, waiting for transfers between devices, per_device(): lax.all_to_all(made[0], 'dp', split_axis=0, concat_axis=1, tiled=True)  9.37 us
    all_gather x1, blocking collectives, gather_and_add(): shards = lax.all_gather(x, axis)  6.95 us
    all_gather x1, blocking collectives, per_device(): hidden = lax.all_gather(hidden_part, 'mp', axis=1, tiled=True)  5.2 us
    all_to_all x1, starting transfers between devices, per_device(): lax.all_to_all(made[1], 'dp', split_axis=0, concat_axis=1, tiled=True)  3.67 us
  transfers between devices with their start and end apart: 4, of which 3 were waited for; matrix products, arithmetic and copies ran while one was open for 11% of the time, Pallas kernels for 0%

profile of v1, /device:TPU:0, one launch (start us, length us, event | category | flops | bytes accessed | tf_op | source)
XLA Modules:
  0.0 163.5 jit_solution(2229031257675506405)
XLA Ops:
  6.5 0.7 all-gather.3.cloned.1.call-update
  7.3 0.0 reduce-scatter.2.cloned.1.call-start
  7.3 0.7 convert_element_type.47
  8.0 38.1 %all-gather.3.cloned.1.call-done = bf16[1024,2048]{1,0:T(8,128)(2,1)} async-done(((bf16[1024,512]{1,0:T(8,128)(2,1)}), bf16[1024,2048]{1,0:T(8,128)(2,1)}) %all-gather.3.cloned.1.call-update) | async-done | bytes 4194320 | tf_op jit(solution)/shard_map/all_gather | solution.py:49
  46.1 3.1 %fusion = f32[1024]{0:T(1024)S(1)} fusion(bf16[1024,2048]{1,0:T(8,128)(2,1)} %all-gather.3.cloned.1.call-done), kind=kLoop, calls=%fused_computation.3 | loop fusion | flops 6290432 | bytes 4198400 | tf_op jit(solution)/shard_map/reduce_sum | solution.py:51
  49.2 10.7 %fusion.16 = f32[1024,1280]{1,0:T(8,128)} fusion(bf16[2048,1280]{1,0:T(8,128)(2,1)} %param.14, bf16[1024,2048]{1,0:T(8,128)(2,1)} %all-gather.3.cloned.1.call-done, f32[2048]{0:T(1024)S(1)} %convert_element_type.47, f32[1024]{0:T(1024)S(1)} %add_rsqrt_fusion), kind=kOutput, calls=%fused_computation.23 | convolution fusion | flops 5377097728 | bytes 14692352 | tf_op jit(solution)/shard_map/dot_general | solution.py:15
  59.9 19.9 %convolution_convert_fusion.2 = bf16[1024,2048]{1,0:T(8,128)(2,1)} fusion(bf16[1280,2048]{1,0:T(8,128)(2,1)} %param.16, f32[1024,1280]{1,0:T(8,128)} %fusion.16, bf16[2048,1280]{1,0:T(8,128)(2,1)} %param.15, bf16[1024,2048]{1,0:T(8,128)(2,1)} %all-gather.3.cloned.1.call-done, f32[2048]{0:T(1024)S(1)} %convert_element_type.47, f32[1024]{0:T(1024)S(1)} %add_rsqrt_fusion), kind=kOutput, calls=%fused_computation.20 | convolution fusion | flops 10761011200 | bytes 24129536 | tf_op jit(solution)/shard_map/dot_general | solution.py:15
  79.8 0.0 reduce-scatter.2.cloned.1.call-update
  80.5 0.7 fusion.27
  81.2 0.1 pad.3.clone
  81.3 0.6 dynamic-slice.4
  82.6 0.2 dynamic-update-slice.1
  82.8 11.3 %all-reduce = s32[64]{0:T(128)S(1)} all-reduce(s32[64]{0:T(128)S(1)} %dynamic-update-slice.1), channel_id=1, replica_groups=mesh['dp'=8,'mp'=4] {'dp'}, use_global_device_ids=true, to_apply=%add | all-reduce | flops 64 | bytes 512
  94.2 0.1 fusion.18
  94.3 5.2 %all_gather.17 = bf16[8,1024]{1,0:T(8,128)(2,1)S(1)} all-gather(bf16[8,256]{1,0:T(8,128)(2,1)S(1)} %fusion.18), channel_id=1, replica_groups=mesh['dp'=8,'mp'=4] {'mp'}, dimensions={1}, use_global_device_ids=true | all-gather | bytes 20480 | tf_op jit(solution)/shard_map/all_gather | solution.py:38
  99.5 0.7 gather_fusion
  100.2 5.8 %fusion.12 = bf16[8,8,4096]{2,1,0:T(8,128)(2,1)} fusion(bf16[1024,4096]{1,0:T(8,128)(2,1)} %param.22, bf16[64,1024]{1,0:T(8,128)(2,1)S(1)} %gather_fusion, pred[64]{0:T(512)(128)(4,1)S(1)} %compare_and_fusion), kind=kOutput, calls=%fused_computation.18 | convolution fusion | flops 537198592 | bytes 9044032 | tf_op jit(solution)/shard_map/dot_general | solution.py:15
  106.0 3.5 %all-to-all-start = ((bf16[8,8,4096]{2,1,0:T(8,128)(2,1)}), bf16[8,8,4096]{2,1,0:T(8,128)(2,1)S(1)}, u32[]{:S(2)}, u32[]{:S(2)}) async-start(bf16[8,8,4096]{2,1,0:T(8,128)(2,1)} %fusion.12), calls=%async_computation.1 | async-start | bytes 1048576 | tf_op jit(solution)/shard_map/all_to_all | solution.py:46
  109.5 5.8 %fusion.13 = bf16[8,8,4096]{2,1,0:T(8,128)(2,1)} fusion(bf16[1024,4096]{1,0:T(8,128)(2,1)} %param.23, bf16[64,1024]{1,0:T(8,128)(2,1)S(1)} %gather_fusion, pred[64]{0:T(512)(128)(4,1)S(1)} %compare_and_fusion), kind=kOutput, calls=%fused_computation.19 | convolution fusion | flops 537198592 | bytes 9044032 | tf_op jit(solution)/shard_map/dot_general | solution.py:15
  115.3 9.4 %all-to-all-done = bf16[8,8,4096]{2,1,0:T(8,128)(2,1)S(1)} async-done(((bf16[8,8,4096]{2,1,0:T(8,128)(2,1)}), bf16[8,8,4096]{2,1,0:T(8,128)(2,1)S(1)}, u32[]{:S(2)}, u32[]{:S(2)}) %all-to-all-start) | async-done | bytes 524320 | tf_op jit(solution)/shard_map/all_to_all | solution.py:46
  124.7 3.7 %all-to-all-start.1 = ((bf16[8,8,4096]{2,1,0:T(8,128)(2,1)}), bf16[8,8,4096]{2,1,0:T(8,128)(2,1)S(1)}, u32[]{:S(2)}, u32[]{:S(2)}) async-start(bf16[8,8,4096]{2,1,0:T(8,128)(2,1)} %fusion.13), calls=%async_computation.2 | async-start | bytes 1048576 | tf_op jit(solution)/shard_map/all_to_all | solution.py:47
  128.4 0.3 copy.17
  128.7 2.1 %reshape.46 = bf16[8,512,64]{2,1,0:T(8,128)(2,1)} reshape(bf16[8,8,4096]{2,1,0:T(8,128)(2,1)S(1)} %copy.17) | data formatting | bytes 1048576 | tf_op jit(solution)/shard_map/reshape | solution.py:63
  130.8 12.2 %all-to-all-done.1 = bf16[8,8,4096]{2,1,0:T(8,128)(2,1)S(1)} async-done(((bf16[8,8,4096]{2,1,0:T(8,128)(2,1)}), bf16[8,8,4096]{2,1,0:T(8,128)(2,1)S(1)}, u32[]{:S(2)}, u32[]{:S(2)}) %all-to-all-start.1) | async-done | bytes 524320 | tf_op jit(solution)/shard_map/all_to_all | solution.py:47
  143.0 0.3 copy.19
  143.3 1.1 reshape.47
  144.5 0.0 reduce-scatter.2.cloned.1.call-done
  144.5 2.1 %convolution_convert_fusion.3 = bf16[8,128,64]{1,2,0:T(8,128)(2,1)S(1)} fusion(bf16[8,128,512]{2,1,0:T(8,128)(2,1)} %bitcast.26, bf16[8,512,64]{2,1,0:T(8,128)(2,1)} %reshape.46), kind=kOutput, calls=%fused_computation.24 | convolution fusion | flops 67174400 | bytes 1703936 | tf_op jit(solution)/shard_map/std,sdr->str/dot_general | solution.py:66
  146.7 7.0 %all-gather = bf16[32,128,64]{1,2,0:T(8,128)(2,1)} all-gather(bf16[8,128,64]{1,2,0:T(8,128)(2,1)S(1)} %convolution_convert_fusion.3), channel_id=2, replica_groups=mesh['dp'=8,'mp'=4] {'mp'}, dimensions={0}, use_global_device_ids=true | all-gather | bytes 655360 | tf_op jit(solution)/shard_map/all_gather | solution.py:10
  153.6 1.1 reduce_sum.22
  154.7 0.5 fusion.21
  155.3 1.4 fusion.14
  (19 shorter events, 0.1 us)
Async XLA Ops:
  6.5 87.6 %copy-start = (bf16[128,256]{1,0:T(8,128)(2,1)S(1)}, bf16[128,256]{1,0:T(8,128)(2,1)}, u32[]{:S(2)}) copy-start(bf16[128,256]{1,0:T(8,128)(2,1)} %param.21) | copy-start | bytes 196612
  6.5 39.6 %all-gather.3.cloned.1.call-start = ((), (), s32[]{:S(2)}) async-start(), calls=%async_computation.3 | async-start | bytes 5242880 | tf_op jit(solution)/shard_map/all_gather | solution.py:49
  7.3 137.2 %reduce-scatter.2.cloned.1.call-start = ((), (), s32[]{:S(2)}) async-start(), calls=%async_computation.4 | async-start | bytes 5242880 | tf_op jit(solution)/shard_map/reduce_scatter | solution.py:60
  59.9 20.6 %copy-start.3 = (f32[8,64]{1,0:T(8,128)S(1)}, f32[8,64]{1,0:T(8,128)}, u32[]{:S(2)}) copy-start(f32[8,64]{1,0:T(8,128)} %param.17) | copy-start | bytes 6148
  59.9 21.4 %copy-start.5 = (u32[32]{0:T(128)S(1)}, u32[32]{0:T(128)}, u32[]{:S(2)}) copy-start(u32[32]{0:T(128)} %constant.75) | copy-start | bytes 388
  59.9 22.7 %copy-start.4 = (s32[8]{0:T(128)S(1)}, s32[8]{0:T(128)}, u32[]{:S(2)}) copy-start(s32[8]{0:T(128)} %param.19) | copy-start | bytes 100
  106.0 18.7 %all-to-all-start = ((bf16[8,8,4096]{2,1,0:T(8,128)(2,1)}), bf16[8,8,4096]{2,1,0:T(8,128)(2,1)S(1)}, u32[]{:S(2)}, u32[]{:S(2)}) async-start(bf16[8,8,4096]{2,1,0:T(8,128)(2,1)} %fusion.12), calls=%async_computation.1 | async-start | bytes 1048576 | tf_op jit(solution)/shard_map/all_to_all | solution.py:46
  124.7 18.3 %all-to-all-start.1 = ((bf16[8,8,4096]{2,1,0:T(8,128)(2,1)}), bf16[8,8,4096]{2,1,0:T(8,128)(2,1)S(1)}, u32[]{:S(2)}, u32[]{:S(2)}) async-start(bf16[8,8,4096]{2,1,0:T(8,128)(2,1)} %fusion.13), calls=%async_computation.2 | async-start | bytes 1048576 | tf_op jit(solution)/shard_map/all_to_all | solution.py:47
  128.7 26.5 %copy-start.1 = (bf16[1024,512]{1,0:T(8,128)(2,1)S(1)}, bf16[1024,512]{1,0:T(8,128)(2,1)}, u32[]{:S(2)}) copy-start(bf16[1024,512]{1,0:T(8,128)(2,1)} %param.12) | copy-start | bytes 3145732
  144.5 10.7 %copy-start.2 = (bf16[1024,512]{1,0:T(8,128)(2,1)S(1)}, bf16[1024,512]{1,0:T(8,128)(2,1)}, u32[]{:S(2)}) copy-start(bf16[1024,512]{1,0:T(8,128)(2,1)} %reduce-scatter.2.cloned.1.call-done) | copy-start | bytes 3145732
Sparse Core Ops, SparseCore 0:
  8.9 37.1 all-gather.2
  80.0 44.3 reduce-scatter.1
